TPU v7x, 32 devices: a whole 2x2x4 slice. The times are simulated.
32 devices in a mesh: stack: 2 (over y), date: 4 (over x, core), line: 4 (over z).
Axes of the slice: x: 2, y: 2, z: 4, core: 2. Of those that a mesh axis runs over, the one named last changes fastest.
Arguments:
- slc: float32 [4, 2, 512, 1280], P('date', None, 'stack', 'line'), parts along dimension 2, may hold values from -6 to 6
- band_start: int32 [4], replicated, may hold values from 0 to 640, as said below
- band_stop: int32 [4], replicated, may hold values from 640 to 1280, as said below
Outputs:
- interferogram: float32 [4, 2, 512, 256], P('date', None, 'stack', 'line'), parts along dimension 2
There are 2 independent parts, one for each index of `stack`. A program takes and returns all parts, laid end to end along the dimension named above; an argument that names none is the same for every part. Nothing has to cross between parts.
Inputs may be any that keep to these rules, and one draw needn't show every extreme that they name: For every pair, band_stop - band_start lies between 640 and 960; at least one pair keeps exactly 960 bins, and some pair keeps exactly 640 bins ending at 1280. `band_stop`: see band_start.
All inputs are finite; a program needn't handle non-finite values.
Results may differ from a plain program's by a relative error of at most 0.0001.
Values sent between devices are 32-bit elements; how exact they have to be, the bound alone decides.
No kernel may reach another device: no remote copies, remote signals or barrier semaphores. Data moves between devices by JAX's collectives and lax.ppermute only.
A program may use at most 64 MiB of HBM per device.

v0:
```python
import functools
import math

import jax
import jax.numpy as jnp
import numpy as np
from jax import lax
from jax.experimental import pallas as pl
from jax.experimental.pallas import tpu as pltpu
from jax.sharding import PartitionSpec as P


LOOKS = 5
LANES = 128
MIB = 1 << 20
HALF = LANES // 2


HIGHEST_PRECISION = lax.Precision.HIGHEST


def shifted(shard, axis, by):
    size = lax.axis_size(axis)
    return lax.ppermute(shard, axis, [(i, (i + by) % size) for i in range(size)])


def phase_table(count, sign_value):
    index_row = jnp.arange(count, dtype=jnp.int32)
    wrapped = index_row[:, None] * index_row[None, :] % count
    angle_all = 2.0 * math.pi / count * wrapped.astype(jnp.float32)
    return (jnp.cos(angle_all), sign_value * jnp.sin(angle_all))


def twiddle_table(outer, inner, sign_value):
    outer_row = jnp.arange(outer, dtype=jnp.int32)
    inner_row = jnp.arange(inner, dtype=jnp.int32)
    wrapped = outer_row[:, None] * inner_row[None, :] % (outer * inner)
    angle_all = 2.0 * math.pi / (outer * inner) * wrapped.astype(jnp.float32)
    return (jnp.cos(angle_all), sign_value * jnp.sin(angle_all))


def left_product(table_real, table_imag, data_real, data_imag):

    def single(table, data):
        return jnp.einsum("ka,cab->ckb", table, data, precision=HIGHEST_PRECISION)

    return (
        single(table_real, data_real) - single(table_imag, data_imag),
        single(table_real, data_imag) + single(table_imag, data_real),
    )


def right_product(data_real, data_imag, table_real, table_imag):

    def single(data, table):
        return jnp.einsum("ckb,bm->ckm", data, table, precision=HIGHEST_PRECISION)

    return (
        single(data_real, table_real) - single(data_imag, table_imag),
        single(data_imag, table_real) + single(data_real, table_imag),
    )


def forward_dft(data_real, data_imag):
    outer = data_real.shape[1]
    inner = data_real.shape[2]
    outer_real, outer_imag = phase_table(outer, -1.0)
    first_real, first_imag = left_product(outer_real, outer_imag, data_real, data_imag)
    twist_real, twist_imag = twiddle_table(outer, inner, -1.0)
    turned_real = first_real * twist_real - first_imag * twist_imag
    turned_imag = first_real * twist_imag + first_imag * twist_real
    inner_real, inner_imag = phase_table(inner, -1.0)
    return right_product(turned_real, turned_imag, inner_real, inner_imag)


def inverse_dft(data_real, data_imag):
    outer = data_real.shape[1]
    inner = data_real.shape[2]
    inner_real, inner_imag = phase_table(inner, 1.0)
    first_real, first_imag = right_product(data_real, data_imag, inner_real, inner_imag)
    twist_real, twist_imag = twiddle_table(outer, inner, 1.0)
    turned_real = first_real * twist_real - first_imag * twist_imag
    turned_imag = first_real * twist_imag + first_imag * twist_real
    outer_real, outer_imag = phase_table(outer, 1.0)
    result_real, result_imag = left_product(outer_real, outer_imag, turned_real, turned_imag)
    scale = 1.0 / (outer * inner)
    return (result_real * scale, result_imag * scale)


def conj_product(ref_real, ref_imag, sec_real, sec_imag):
    return (ref_real * sec_real + ref_imag * sec_imag, ref_imag * sec_real - ref_real * sec_imag)


def look_mean(values):
    return values.reshape(values.shape[0], values.shape[1] // LOOKS, LOOKS).sum(axis=-1) * (
        1.0 / LOOKS
    )


def general_shards(slc, band_start, band_stop):
    own_image = slc[0]
    line_lines = own_image.shape[2]
    turned = lax.all_to_all(own_image, "line", split_axis=1, concat_axis=2, tiled=True)
    columns = turned.shape[1]
    outer = lax.axis_size("line")
    lines_all = outer * line_lines
    blocks = turned.reshape(2, columns, outer, line_lines)
    spec_real, spec_imag = forward_dft(blocks[0], blocks[1])
    spectrum = jnp.stack([spec_real, spec_imag], axis=0)
    date_index = lax.axis_index("date")
    my_start = lax.dynamic_slice_in_dim(band_start, date_index, 1)[0]
    my_end = lax.dynamic_slice_in_dim(band_stop, date_index, 1)[0]
    bin_index = (
        jnp.arange(outer, dtype=jnp.int32)[:, None]
        + outer * jnp.arange(line_lines, dtype=jnp.int32)[None, :]
    )
    keep_mask = ((bin_index >= my_start) & (bin_index < my_end)).astype(jnp.float32)
    partner = shifted(spectrum, "date", -1)
    ref_spec = spectrum * keep_mask
    sec_spec = partner * keep_mask
    both_real, both_imag = inverse_dft(
        jnp.concatenate([ref_spec[0], sec_spec[0]], axis=0),
        jnp.concatenate([ref_spec[1], sec_spec[1]], axis=0),
    )
    ref_real = both_real[:columns].reshape(columns, lines_all)
    ref_imag = both_imag[:columns].reshape(columns, lines_all)
    sec_real = both_real[columns:].reshape(columns, lines_all)
    sec_imag = both_imag[columns:].reshape(columns, lines_all)
    prod_real, prod_imag = conj_product(ref_real, ref_imag, sec_real, sec_imag)
    looked = jnp.stack([look_mean(prod_real), look_mean(prod_imag)], axis=0)
    result = lax.all_to_all(looked, "line", split_axis=2, concat_axis=1, tiled=True)
    return result[None]


def split_pair(values):
    high = values.astype(jnp.bfloat16)
    low = (values - high.astype(jnp.float32)).astype(jnp.bfloat16)
    return high, low


@functools.lru_cache(maxsize=None)
def host_tables(inner):
    index = np.arange(inner)
    angle = 2.0 * np.pi * ((index[:, None] * index[None, :]) % inner) / inner
    both = np.concatenate([np.cos(angle), np.sin(angle)], axis=1)
    high = both.astype(jnp.bfloat16)
    low = (both - high.astype(np.float64)).astype(jnp.bfloat16)
    matrix = np.stack([high, low])
    turn = 2.0 * np.pi * np.arange(1, LOOKS)[:, None] * index[None, :] / (LOOKS * inner)
    twist = np.stack([np.cos(turn), np.sin(turn)], axis=1).astype(np.float32)
    twist = np.broadcast_to(twist[..., None], (LOOKS - 1, 2, inner, LANES))
    return matrix, np.ascontiguousarray(twist)


def low_lanes(shape):
    return lax.broadcasted_iota(jnp.int32, shape, len(shape) - 1) < HALF


def swap_halves(values):
    return pltpu.roll(values, HALF, values.ndim - 1)


def pack_kernel(peers, image_ref, *chunk_refs):
    me = lax.axis_index("line")
    side = me % 2
    for pair in range(peers // 2):
        block = jnp.bitwise_xor(me // 2, pair)
        lane = pl.multiple_of(block * LANES, LANES)
        real = image_ref[0, :, pl.ds(lane, LANES)]
        imag = image_ref[1, :, pl.ds(lane, LANES)]
        mask = low_lanes(real.shape)
        first = jnp.where(mask, real, swap_halves(imag))
        second = jnp.where(mask, swap_halves(real), imag)
        chunk_refs[2 * pair][...] = jnp.where(side == 0, first, second)
        chunk_refs[2 * pair + 1][...] = jnp.where(side == 0, second, first)


COS1, COS2 = math.cos(2.0 * math.pi / 5), math.cos(4.0 * math.pi / 5)
SIN1, SIN2 = math.sin(2.0 * math.pi / 5), math.sin(4.0 * math.pi / 5)


def five_point(real, imag, sign):
    sum_r1, sum_i1 = real[1] + real[4], imag[1] + imag[4]
    sum_r2, sum_i2 = real[2] + real[3], imag[2] + imag[3]
    dif_r1, dif_i1 = real[1] - real[4], imag[1] - imag[4]
    dif_r2, dif_i2 = real[2] - real[3], imag[2] - imag[3]
    out_r0, out_i0 = real[0] + sum_r1 + sum_r2, imag[0] + sum_i1 + sum_i2
    even_r1 = real[0] + COS1 * sum_r1 + COS2 * sum_r2
    even_i1 = imag[0] + COS1 * sum_i1 + COS2 * sum_i2
    even_r2 = real[0] + COS2 * sum_r1 + COS1 * sum_r2
    even_i2 = imag[0] + COS2 * sum_i1 + COS1 * sum_i2
    odd_r1 = (sign * SIN1) * dif_r1 + (sign * SIN2) * dif_r2
    odd_i1 = (sign * SIN1) * dif_i1 + (sign * SIN2) * dif_i2
    odd_r2 = (sign * SIN2) * dif_r1 - (sign * SIN1) * dif_r2
    odd_i2 = (sign * SIN2) * dif_i1 - (sign * SIN1) * dif_i2
    return (
        [out_r0, even_r1 - odd_i1, even_r2 - odd_i2, even_r2 + odd_i2, even_r1 + odd_i1],
        [out_i0, even_i1 + odd_r1, even_i2 + odd_r2, even_i2 - odd_r2, even_i1 - odd_r1],
    )


def main_kernel(peers, inner, start_ref, stop_ref, matrix_ref, twist_ref, *refs):
    own_refs, sec_refs = refs[:peers], refs[peers : 2 * peers]
    out_refs = refs[2 * peers : 3 * peers]
    real_ref, imag_ref, mid_ref, high_ref, low_ref, sum_ref = refs[3 * peers :]
    me = lax.axis_index("line")
    date = lax.axis_index("date")
    chunk_lines = own_refs[0].shape[0]
    lines_all = peers * chunk_lines
    for r in range(peers):
        base = pl.multiple_of(jnp.bitwise_xor(me, r) * chunk_lines, 8)
        own, sec = own_refs[r][...], sec_refs[r][...]
        mask = low_lanes(own.shape)
        real_ref[pl.ds(base, chunk_lines), :] = jnp.where(mask, own, swap_halves(sec))
        imag_ref[pl.ds(base, chunk_lines), :] = jnp.where(mask, swap_halves(own), sec)

    high_table, low_table = matrix_ref[0], matrix_ref[1]

    def transform(high, low):
        return (
            jnp.dot(high_table, high, preferred_element_type=jnp.float32)
            + jnp.dot(high_table, low, preferred_element_type=jnp.float32)
            + jnp.dot(low_table, high, preferred_element_type=jnp.float32)
        )

    for l in range(LOOKS):
        real_high, real_low = split_pair(real_ref[pl.ds(l, inner, stride=LOOKS), :])
        imag_high, imag_low = split_pair(imag_ref[pl.ds(l, inner, stride=LOOKS), :])
        high = jnp.concatenate(
            [
                jnp.concatenate([real_high, imag_high], axis=1),
                jnp.concatenate([imag_high, -real_high], axis=1),
            ],
            axis=0,
        )
        low = jnp.concatenate(
            [
                jnp.concatenate([real_low, imag_low], axis=1),
                jnp.concatenate([imag_low, -real_low], axis=1),
            ],
            axis=0,
        )
        mid_ref[l] = transform(high, low)

    start, stop = start_ref[date], stop_ref[date]
    rows = 16

    def spectral(step, carry):
        row = pl.multiple_of(step * rows, rows)
        span = pl.ds(row, rows)
        real = [mid_ref[l, span, :LANES] for l in range(LOOKS)]
        imag = [mid_ref[l, span, LANES:] for l in range(LOOKS)]
        turn = [(twist_ref[l, 0, span, :], twist_ref[l, 1, span, :]) for l in range(LOOKS - 1)]
        for l in range(1, LOOKS):
            c, s = turn[l - 1]
            real[l], imag[l] = real[l] * c + imag[l] * s, imag[l] * c - real[l] * s
        real, imag = five_point(real, imag, -1.0)
        first = lax.broadcasted_iota(jnp.int32, (rows, LANES), 0) + row
        for m in range(LOOKS):
            bin_index = first + m * inner
            keep = (bin_index >= start) & (bin_index < stop)
            weight = jnp.where(keep, 1.0 / lines_all, 0.0)
            real[m], imag[m] = real[m] * weight, imag[m] * weight
        real, imag = five_point(real, imag, 1.0)
        for l in range(1, LOOKS):
            c, s = turn[l - 1]
            real[l], imag[l] = real[l] * c - imag[l] * s, imag[l] * c + real[l] * s
        span_below = pl.ds(pl.multiple_of(row + inner, rows), rows)
        for l in range(LOOKS):
            real_high, real_low = split_pair(real[l])
            imag_high, imag_low = split_pair(imag[l])
            high_ref[l, span, :LANES] = real_high
            high_ref[l, span, LANES:] = imag_high
            high_ref[l, span_below, :LANES] = -imag_high
            high_ref[l, span_below, LANES:] = real_high
            low_ref[l, span, :LANES] = real_low
            low_ref[l, span, LANES:] = imag_low
            low_ref[l, span_below, :LANES] = -imag_low
            low_ref[l, span_below, LANES:] = real_low
        return carry

    lax.fori_loop(0, inner // rows, spectral, 0)

    total = None
    for l in range(LOOKS):
        signal = transform(high_ref[l], low_ref[l])
        real, imag = signal[:, :LANES], signal[:, LANES:]
        real_other, imag_other = swap_halves(real), swap_halves(imag)
        product = jnp.where(
            low_lanes(real.shape),
            real * real_other + imag * imag_other,
            real * imag_other - imag * real_other,
        )
        total = product if total is None else total + product
    sum_ref[...] = total * (1.0 / LOOKS)
    out_lines = inner // peers
    for r in range(peers):
        base = pl.multiple_of(jnp.bitwise_xor(me, r) * out_lines, 8)
        out_refs[r][...] = sum_ref[pl.ds(base, out_lines), :]


def unpack_kernel(peers, *refs):
    chunk_refs, out_ref = refs[:peers], refs[peers]
    me = lax.axis_index("line")
    side = me % 2
    for pair in range(peers // 2):
        block = jnp.bitwise_xor(me // 2, pair)
        lane = pl.multiple_of(block * LANES, LANES)
        even, odd = chunk_refs[2 * pair][...], chunk_refs[2 * pair + 1][...]
        first = jnp.where(side == 0, even, odd)
        second = jnp.where(side == 0, odd, even)
        mask = low_lanes(first.shape)
        out_ref[0, :, pl.ds(lane, LANES)] = jnp.where(mask, first, swap_halves(second))
        out_ref[1, :, pl.ds(lane, LANES)] = jnp.where(mask, swap_halves(first), second)


def packed_step(slc, band_start, band_stop):
    peers = lax.axis_size("line")
    chunk_lines = slc.shape[3]
    inner = peers * chunk_lines // LOOKS
    out_lines = inner // peers
    f32 = jnp.float32
    vmem = pl.BlockSpec(memory_space=pltpu.VMEM)
    smem = pl.BlockSpec(memory_space=pltpu.SMEM)
    chunk = jax.ShapeDtypeStruct((chunk_lines, LANES), f32)
    image = jnp.transpose(slc[0], (0, 2, 1))
    packed = pl.pallas_call(
        functools.partial(pack_kernel, peers),
        out_shape=[chunk] * peers,
        in_specs=[vmem],
        out_specs=[vmem] * peers,
        compiler_params=pltpu.CompilerParams(vmem_limit_bytes=8 * MIB),
        name="pack",
    )(image)

    def exchange(values, r):
        return lax.ppermute(values, "line", [(i, i ^ r) for i in range(peers)])

    def forward(values):
        return shifted(values, "date", -1)

    own = [values if r == 0 else exchange(values, r) for r, values in enumerate(packed)]
    sec = [forward(values) for values in own]
    matrix, twist = host_tables(inner)
    looked = pl.pallas_call(
        functools.partial(main_kernel, peers, inner),
        out_shape=[jax.ShapeDtypeStruct((out_lines, LANES), f32)] * peers,
        in_specs=[smem, smem, vmem, vmem] + [vmem] * (2 * peers),
        out_specs=[vmem] * peers,
        scratch_shapes=[
            pltpu.VMEM((peers * chunk_lines, LANES), f32),
            pltpu.VMEM((peers * chunk_lines, LANES), f32),
            pltpu.VMEM((LOOKS, inner, 2 * LANES), f32),
            pltpu.VMEM((LOOKS, 2 * inner, 2 * LANES), jnp.bfloat16),
            pltpu.VMEM((LOOKS, 2 * inner, 2 * LANES), jnp.bfloat16),
            pltpu.VMEM((inner, LANES), f32),
        ],
        compiler_params=pltpu.CompilerParams(vmem_limit_bytes=24 * MIB),
        name="interfere",
    )(band_start, band_stop, jnp.asarray(matrix), jnp.asarray(twist), *own, *sec)
    looked = [values if r == 0 else exchange(values, r) for r, values in enumerate(looked)]
    result = pl.pallas_call(
        functools.partial(unpack_kernel, peers),
        out_shape=jax.ShapeDtypeStruct((2, out_lines, slc.shape[2]), f32),
        in_specs=[vmem] * peers,
        out_specs=vmem,
        compiler_params=pltpu.CompilerParams(vmem_limit_bytes=8 * MIB),
        name="unpack",
    )(*looked)
    return jnp.transpose(result, (0, 2, 1))[None]


def packs(mesh, slc):
    peers = mesh.shape["line"]
    columns = slc.shape[2] // mesh.shape["stack"] // peers
    chunk_lines = slc.shape[3] // peers
    inner = slc.shape[3] // LOOKS
    return (
        peers > 1
        and peers & (peers - 1) == 0
        and columns == HALF
        and chunk_lines % 8 == 0
        and inner % (8 * peers) == 0
        and inner % LANES == 0
        and inner <= 4 * LANES
    )


def solution(mesh):
    specs = dict(
        mesh=mesh,
        in_specs=(P("date", None, "stack", "line"), P(), P()),
        out_specs=P("date", None, "stack", "line"),
        check_vma=False,
    )

    def whole(slc, band_start, band_stop):
        if not packs(mesh, slc):
            return jax.shard_map(general_shards, **specs)(slc, band_start, band_stop)
        step = jax.shard_map(packed_step, **specs)
        return step(slc, band_start, band_stop)

    return whole
```

profile of v0, /device:TPU:0, one launch (start us, length us, event | category | flops | bytes accessed | tf_op | source)
XLA Modules:
  0.0 39.8 jit_solution(10974719542927030553)
XLA Ops:
  0.0 0.0 copy-start.1
  0.0 1.1 %copy-done.1 = f32[1,2,256,320]{2,3,1,0:T(8,128)S(1)} copy-done((f32[1,2,256,320]{2,3,1,0:T(8,128)S(1)}, f32[1,2,256,320]{2,3,1,0:T(8,128)}, u32[]{:S(2)}) %copy-start.1) | copy-done | bytes 655384
  1.1 0.0 copy-start.2
  1.1 0.2 pack.1
  1.3 3.1 %collective-permute-start = (f32[320,128]{1,0:T(8,128)S(1)}, f32[320,128]{1,0:T(8,128)S(1)}, u32[]{:S(2)}, u32[]{:S(2)}) collective-permute-start(f32[320,128]{1,0:T(8,128)S(1)} %get-tuple-element.14), channel_id=1, source_target_pairs={{0,1},{1,0},{2,3},{3,2},{4,5},{5,4},{6,7},{7,6},{8,9},{9,8},{10,11... | collective-permute-start | bytes 491528 | tf_op jit(solution)/shard_map/ppermute | solution.py:337
  4.5 2.6 %collective-permute-start.1 = (f32[320,128]{1,0:T(8,128)S(1)}, f32[320,128]{1,0:T(8,128)S(1)}, u32[]{:S(2)}, u32[]{:S(2)}) collective-permute-start(f32[320,128]{1,0:T(8,128)S(1)} %get-tuple-element.15), channel_id=1, source_target_pairs={{0,2},{1,3},{2,0},{3,1},{4,6},{5,7},{6,4},{7,5},{8,10},{9,11},{10,... | collective-permute-start | bytes 491528 | tf_op jit(solution)/shard_map/ppermute | solution.py:337
  7.0 0.0 copy-start.3
  7.0 0.0 copy-start.4
  7.0 0.0 collective-permute-start.2
  7.0 0.4 collective-permute-start.3
  7.4 3.7 %collective-permute-done.refs_1_ = f32[320,128]{1,0:T(8,128)S(1)} collective-permute-done((f32[320,128]{1,0:T(8,128)S(1)}, f32[320,128]{1,0:T(8,128)S(1)}, u32[]{:S(2)}, u32[]{:S(2)}) %collective-permute-start) | collective-permute-done | bytes 163872 | tf_op jit(solution)/shard_map/ppermute | solution.py:337
  11.2 0.0 collective-permute-start.4
  11.2 8.3 %collective-permute-done.1.refs_2_ = f32[320,128]{1,0:T(8,128)S(1)} collective-permute-done((f32[320,128]{1,0:T(8,128)S(1)}, f32[320,128]{1,0:T(8,128)S(1)}, u32[]{:S(2)}, u32[]{:S(2)}) %collective-permute-start.1) | collective-permute-done | bytes 163872 | tf_op jit(solution)/shard_map/ppermute | solution.py:337
  19.4 0.0 collective-permute-start.5
  19.4 0.0 collective-permute-done.2.refs_3_
  19.5 1.6 %collective-permute-start.6 = (f32[320,128]{1,0:T(8,128)S(1)}, f32[320,128]{1,0:T(8,128)S(1)}, u32[]{:S(2)}, u32[]{:S(2)}) collective-permute-start(f32[320,128]{1,0:T(8,128)S(1)} %collective-permute-done.2.refs_3_), channel_id=1, source_target_pairs={{0,12},{4,0},{8,4},{12,8},{1,13},{5,1},{9,5},{13,9},{2,14},{6,2},{... | collective-permute-start | bytes 491528 | tf_op jit(solution)/shard_map/ppermute | solution.py:24
  21.1 0.0 collective-permute-done.3.refs_4_
  21.1 0.0 collective-permute-done.4.refs_5_
  21.1 1.2 %collective-permute-done.5.refs_6_ = f32[320,128]{1,0:T(8,128)S(1)} collective-permute-done((f32[320,128]{1,0:T(8,128)S(1)}, f32[320,128]{1,0:T(8,128)S(1)}, u32[]{:S(2)}, u32[]{:S(2)}) %collective-permute-start.5) | collective-permute-done | bytes 163872 | tf_op jit(solution)/shard_map/ppermute | solution.py:24
  22.3 1.8 %collective-permute-done.6.refs_7_ = f32[320,128]{1,0:T(8,128)S(1)} collective-permute-done((f32[320,128]{1,0:T(8,128)S(1)}, f32[320,128]{1,0:T(8,128)S(1)}, u32[]{:S(2)}, u32[]{:S(2)}) %collective-permute-start.6) | collective-permute-done | bytes 163872 | tf_op jit(solution)/shard_map/ppermute | solution.py:24
  24.0 0.0 copy-done.2
  24.0 0.0 copy-done.3
  24.0 0.0 copy-done.4
  24.1 0.0 copy-start
  24.1 1.2 %copy-done = f32[4,2,256,128]{3,2,1,0:T(8,128)S(1)} copy-done((f32[4,2,256,128]{3,2,1,0:T(8,128)S(1)}, f32[4,2,256,128]{3,2,1,0:T(8,128)}, u32[]{:S(2)}) %copy-start) | copy-done | bytes 1048600
  25.3 5.0 %interfere.1 = (f32[64,128]{1,0:T(8,128)S(1)}, f32[64,128]{1,0:T(8,128)S(1)}, f32[64,128]{1,0:T(8,128)S(1)}, f32[64,128]{1,0:T(8,128)S(1)}) custom-call(s32[4]{0:T(128)S(1)} %copy-done.3, s32[4]{0:T(128)S(1)} %copy-done.4, bf16[2,256,512]{2,1,0:T(8,128)(2,1)S(1)} %copy-done.2, f32[4,2,256,128]{3,2,1,0:T(8,128)S(1)} %copy-done, ...), custom_call_target="tpu_custom_call" | custom-call | tf_op jit(solution)/shard_map/interfere/pallas_call | solution.py:345
  30.3 1.0 %collective-permute-start.7 = (f32[64,128]{1,0:T(8,128)S(1)}, f32[64,128]{1,0:T(8,128)S(1)}, u32[]{:S(2)}, u32[]{:S(2)}) collective-permute-start(f32[64,128]{1,0:T(8,128)S(1)} %get-tuple-element.18), channel_id=1, source_target_pairs={{0,1},{1,0},{2,3},{3,2},{4,5},{5,4},{6,7},{7,6},{8,9},{9,8},{10,11... | collective-permute-start | bytes 98312 | tf_op jit(solution)/shard_map/ppermute | solution.py:337
  31.3 1.9 %collective-permute-start.8 = (f32[64,128]{1,0:T(8,128)S(1)}, f32[64,128]{1,0:T(8,128)S(1)}, u32[]{:S(2)}, u32[]{:S(2)}) collective-permute-start(f32[64,128]{1,0:T(8,128)S(1)} %get-tuple-element.19), channel_id=1, source_target_pairs={{0,2},{1,3},{2,0},{3,1},{4,6},{5,7},{6,4},{7,5},{8,10},{9,11},{10,... | collective-permute-start | bytes 98312 | tf_op jit(solution)/shard_map/ppermute | solution.py:337
  33.3 1.5 %collective-permute-start.9 = (f32[64,128]{1,0:T(8,128)S(1)}, f32[64,128]{1,0:T(8,128)S(1)}, u32[]{:S(2)}, u32[]{:S(2)}) collective-permute-start(f32[64,128]{1,0:T(8,128)S(1)} %get-tuple-element.20), channel_id=1, source_target_pairs={{0,3},{1,2},{2,1},{3,0},{4,7},{5,6},{6,5},{7,4},{8,11},{9,10},{10,... | collective-permute-start | bytes 98312 | tf_op jit(solution)/shard_map/ppermute | solution.py:337
  34.8 0.0 collective-permute-done.7.refs_1_
  34.8 1.4 %collective-permute-done.8.refs_2_ = f32[64,128]{1,0:T(8,128)S(1)} collective-permute-done((f32[64,128]{1,0:T(8,128)S(1)}, f32[64,128]{1,0:T(8,128)S(1)}, u32[]{:S(2)}, u32[]{:S(2)}) %collective-permute-start.8) | collective-permute-done | bytes 32800 | tf_op jit(solution)/shard_map/ppermute | solution.py:337
  36.1 2.9 %collective-permute-done.9.refs_3_ = f32[64,128]{1,0:T(8,128)S(1)} collective-permute-done((f32[64,128]{1,0:T(8,128)S(1)}, f32[64,128]{1,0:T(8,128)S(1)}, u32[]{:S(2)}, u32[]{:S(2)}) %collective-permute-start.9) | collective-permute-done | bytes 32800 | tf_op jit(solution)/shard_map/ppermute | solution.py:337
  39.1 0.8 %unpack.1 = f32[2,64,256]{2,1,0:T(8,128)} custom-call(f32[64,128]{1,0:T(8,128)S(1)} %get-tuple-element.17.refs_0_, f32[64,128]{1,0:T(8,128)S(1)} %collective-permute-done.7.refs_1_, f32[64,128]{1,0:T(8,128)S(1)} %collective-permute-done.8.refs_2_, f32[64,128]{1,0:T(8,128)S(1)} %collective-permute-done.9.refs_3_), custom_call_target="tpu_custom_call" | custom-call | tf_op jit(solution)/shard_map/unpack/pallas_call | solution.py:362
Async XLA Ops:
  0.0 1.1 %copy-start.1 = (f32[1,2,256,320]{2,3,1,0:T(8,128)S(1)}, f32[1,2,256,320]{2,3,1,0:T(8,128)}, u32[]{:S(2)}) copy-start(f32[1,2,256,320]{2,3,1,0:T(8,128)} %param.5) | copy-start | bytes 1966084
  1.1 23.0 %copy-start.2 = (bf16[2,256,512]{2,1,0:T(8,128)(2,1)S(1)}, bf16[2,256,512]{2,1,0:T(8,128)(2,1)}, u32[]{:S(2)}) copy-start(bf16[2,256,512]{2,1,0:T(8,128)(2,1)} %constant.4.clone.matrix_ref) | copy-start | bytes 1572868
  1.3 9.8 %collective-permute-start = (f32[320,128]{1,0:T(8,128)S(1)}, f32[320,128]{1,0:T(8,128)S(1)}, u32[]{:S(2)}, u32[]{:S(2)}) collective-permute-start(f32[320,128]{1,0:T(8,128)S(1)} %get-tuple-element.14), channel_id=1, source_target_pairs={{0,1},{1,0},{2,3},{3,2},{4,5},{5,4},{6,7},{7,6},{8,9},{9,8},{10,11... | collective-permute-start | bytes 491528 | tf_op jit(solution)/shard_map/ppermute | solution.py:337
  4.5 15.0 %collective-permute-start.1 = (f32[320,128]{1,0:T(8,128)S(1)}, f32[320,128]{1,0:T(8,128)S(1)}, u32[]{:S(2)}, u32[]{:S(2)}) collective-permute-start(f32[320,128]{1,0:T(8,128)S(1)} %get-tuple-element.15), channel_id=1, source_target_pairs={{0,2},{1,3},{2,0},{3,1},{4,6},{5,7},{6,4},{7,5},{8,10},{9,11},{10,... | collective-permute-start | bytes 491528 | tf_op jit(solution)/shard_map/ppermute | solution.py:337
  7.0 17.0 %copy-start.3 = (s32[4]{0:T(128)S(1)}, s32[4]{0:T(128)}, u32[]{:S(2)}) copy-start(s32[4]{0:T(128)} %start_ref.1) | copy-start | bytes 52
  7.0 17.0 %copy-start.4 = (s32[4]{0:T(128)S(1)}, s32[4]{0:T(128)}, u32[]{:S(2)}) copy-start(s32[4]{0:T(128)} %stop_ref.1) | copy-start | bytes 52
  7.0 12.4 %collective-permute-start.2 = (f32[320,128]{1,0:T(8,128)S(1)}, f32[320,128]{1,0:T(8,128)S(1)}, u32[]{:S(2)}, u32[]{:S(2)}) collective-permute-start(f32[320,128]{1,0:T(8,128)S(1)} %get-tuple-element.16), channel_id=1, source_target_pairs={{0,3},{1,2},{2,1},{3,0},{4,7},{5,6},{6,5},{7,4},{8,11},{9,10},{10,... | collective-permute-start | bytes 491528 | tf_op jit(solution)/shard_map/ppermute | solution.py:337
  7.0 14.0 %collective-permute-start.3 = (f32[320,128]{1,0:T(8,128)S(1)}, f32[320,128]{1,0:T(8,128)S(1)}, u32[]{:S(2)}, u32[]{:S(2)}) collective-permute-start(f32[320,128]{1,0:T(8,128)S(1)} %get-tuple-element.13.refs_0_), channel_id=1, source_target_pairs={{0,12},{4,0},{8,4},{12,8},{1,13},{5,1},{9,5},{13,9},{2,14},{6,2},{... | collective-permute-start | bytes 491528 | tf_op jit(solution)/shard_map/ppermute | solution.py:24
  11.2 9.9 %collective-permute-start.4 = (f32[320,128]{1,0:T(8,128)S(1)}, f32[320,128]{1,0:T(8,128)S(1)}, u32[]{:S(2)}, u32[]{:S(2)}) collective-permute-start(f32[320,128]{1,0:T(8,128)S(1)} %collective-permute-done.refs_1_), channel_id=1, source_target_pairs={{0,12},{4,0},{8,4},{12,8},{1,13},{5,1},{9,5},{13,9},{2,14},{6,2},{... | collective-permute-start | bytes 491528 | tf_op jit(solution)/shard_map/ppermute | solution.py:24
  19.4 2.8 %collective-permute-start.5 = (f32[320,128]{1,0:T(8,128)S(1)}, f32[320,128]{1,0:T(8,128)S(1)}, u32[]{:S(2)}, u32[]{:S(2)}) collective-permute-start(f32[320,128]{1,0:T(8,128)S(1)} %collective-permute-done.1.refs_2_), channel_id=1, source_target_pairs={{0,12},{4,0},{8,4},{12,8},{1,13},{5,1},{9,5},{13,9},{2,14},{6,2},{... | collective-permute-start | bytes 491528 | tf_op jit(solution)/shard_map/ppermute | solution.py:24
  19.5 4.6 %collective-permute-start.6 = (f32[320,128]{1,0:T(8,128)S(1)}, f32[320,128]{1,0:T(8,128)S(1)}, u32[]{:S(2)}, u32[]{:S(2)}) collective-permute-start(f32[320,128]{1,0:T(8,128)S(1)} %collective-permute-done.2.refs_3_), channel_id=1, source_target_pairs={{0,12},{4,0},{8,4},{12,8},{1,13},{5,1},{9,5},{13,9},{2,14},{6,2},{... | collective-permute-start | bytes 491528 | tf_op jit(solution)/shard_map/ppermute | solution.py:24
  24.1 1.2 %copy-start = (f32[4,2,256,128]{3,2,1,0:T(8,128)S(1)}, f32[4,2,256,128]{3,2,1,0:T(8,128)}, u32[]{:S(2)}) copy-start(f32[4,2,256,128]{3,2,1,0:T(8,128)} %constant.5.clone.twist_ref) | copy-start | bytes 3145732
  30.3 4.5 %collective-permute-start.7 = (f32[64,128]{1,0:T(8,128)S(1)}, f32[64,128]{1,0:T(8,128)S(1)}, u32[]{:S(2)}, u32[]{:S(2)}) collective-permute-start(f32[64,128]{1,0:T(8,128)S(1)} %get-tuple-element.18), channel_id=1, source_target_pairs={{0,1},{1,0},{2,3},{3,2},{4,5},{5,4},{6,7},{7,6},{8,9},{9,8},{10,11... | collective-permute-start | bytes 98312 | tf_op jit(solution)/shard_map/ppermute | solution.py:337
  31.3 4.8 %collective-permute-start.8 = (f32[64,128]{1,0:T(8,128)S(1)}, f32[64,128]{1,0:T(8,128)S(1)}, u32[]{:S(2)}, u32[]{:S(2)}) collective-permute-start(f32[64,128]{1,0:T(8,128)S(1)} %get-tuple-element.19), channel_id=1, source_target_pairs={{0,2},{1,3},{2,0},{3,1},{4,6},{5,7},{6,4},{7,5},{8,10},{9,11},{10,... | collective-permute-start | bytes 98312 | tf_op jit(solution)/shard_map/ppermute | solution.py:337
  33.3 5.8 %collective-permute-start.9 = (f32[64,128]{1,0:T(8,128)S(1)}, f32[64,128]{1,0:T(8,128)S(1)}, u32[]{:S(2)}, u32[]{:S(2)}) collective-permute-start(f32[64,128]{1,0:T(8,128)S(1)} %get-tuple-element.20), channel_id=1, source_target_pairs={{0,3},{1,2},{2,1},{3,0},{4,7},{5,6},{6,5},{7,4},{8,11},{9,10},{10,... | collective-permute-start | bytes 98312 | tf_op jit(solution)/shard_map/ppermute | solution.py:337
where the time goes:
time: 40 us; the launch traced here: 39.8 us
  waiting for transfers between devices  19.3 us (48%)
  starting transfers between devices  12.1 us (30%)
  Pallas kernels  6.02 us (15%)
  local copies, waits for them, and re-layouts  2.32 us (6%)
    ppermute x6, waiting for transfers between devices, exchange(): return lax.ppermute(values, 'line', [(i, i ^ r) for i in range(peers)])  16.3 us
    ppermute x6, starting transfers between devices, exchange(): return lax.ppermute(values, 'line', [(i, i ^ r) for i in range(peers)])  10.2 us
    pallas_call x1, Pallas kernels, packed_step(): pl.pallas_call(functools.partial(main_kernel, peers, inner), out_shape=[j...  5.02 us
    ppermute x4, waiting for transfers between devices, shifted(): lax.ppermute(shard, axis, [(i, (i + by) % size) for i in range(size)])  2.99 us
    unnamed x10, local copies, waits for them, and re-layouts  2.32 us
    ppermute x4, starting transfers between devices, shifted(): lax.ppermute(shard, axis, [(i, (i + by) % size) for i in range(size)])  1.98 us
  transfers between devices with their start and end apart: 10, of which 6 were waited for; matrix products, arithmetic and copies ran while one was open for 0% of the time, Pallas kernels for 0%

commit v1 on v0

--- a/solution.py
+++ b/solution.py
@@ -11,6 +11,7 @@
 
 
 LOOKS = 5
+TAPS = 2 * LOOKS
 LANES = 128
 MIB = 1 << 20
 HALF = LANES // 2
@@ -139,17 +140,27 @@
 
 
 @functools.lru_cache(maxsize=None)
-def host_tables(inner):
-    index = np.arange(inner)
-    angle = 2.0 * np.pi * ((index[:, None] * index[None, :]) % inner) / inner
-    both = np.concatenate([np.cos(angle), np.sin(angle)], axis=1)
-    high = both.astype(jnp.bfloat16)
-    low = (both - high.astype(np.float64)).astype(jnp.bfloat16)
-    matrix = np.stack([high, low])
-    turn = 2.0 * np.pi * np.arange(1, LOOKS)[:, None] * index[None, :] / (LOOKS * inner)
-    twist = np.stack([np.cos(turn), np.sin(turn)], axis=1).astype(np.float32)
-    twist = np.broadcast_to(twist[..., None], (LOOKS - 1, 2, inner, LANES))
-    return matrix, np.ascontiguousarray(twist)
+def host_tables(inner, chunk_lines, last):
+    lines_all = TAPS * inner
+    bins, steps, taps = np.arange(inner), np.arange(inner), np.arange(TAPS)
+    turns = bins[None, :, None] * (TAPS * steps[None, None, :] + taps[:, None, None]) % lines_all
+    angle = 2.0 * np.pi / lines_all * turns
+    cos, sin = np.cos(angle), np.sin(angle)
+
+    def halves(table):
+        high = table.astype(jnp.bfloat16)
+        low = (table - high.astype(np.float64)).astype(jnp.bfloat16)
+        return high, low
+
+    ahead = halves(np.concatenate([cos, sin], axis=2))
+    swapped = [np.swapaxes(table, 1, 2) for table in (cos, -sin)]
+    back = halves(np.concatenate(swapped, axis=2))
+    few = chunk_lines // TAPS
+    part = slice(last * few, (last + 1) * few)
+    high, low = halves(np.concatenate([cos[:, :, part], sin[:, :, part]], axis=2))
+    late = np.concatenate([high, high, low], axis=2)
+    late = np.pad(late, ((0, 0), (0, 0), (0, -late.shape[2] % (2 * LANES))))
+    return np.stack(ahead), np.stack(back), late
 
 
 def low_lanes(shape):
@@ -199,103 +210,134 @@
     )
 
 
-def main_kernel(peers, inner, start_ref, stop_ref, matrix_ref, twist_ref, *refs):
-    own_refs, sec_refs = refs[:peers], refs[peers : 2 * peers]
-    out_refs = refs[2 * peers : 3 * peers]
-    real_ref, imag_ref, mid_ref, high_ref, low_ref, sum_ref = refs[3 * peers :]
+def ten_point(real, imag, sign):
+    first = [2 * b % TAPS for b in range(LOOKS)]
+    other = [(LOOKS + 2 * b) % TAPS for b in range(LOOKS)]
+    out_real, out_imag = [None] * TAPS, [None] * TAPS
+    for c in range(2):
+        join = (lambda x, y: x - y) if c else (lambda x, y: x + y)
+        part_real = [join(real[i], real[j]) for i, j in zip(first, other)]
+        part_imag = [join(imag[i], imag[j]) for i, j in zip(first, other)]
+        part_real, part_imag = five_point(part_real, part_imag, sign)
+        for m in range(TAPS):
+            if m % 2 == c:
+                out_real[m], out_imag[m] = part_real[m % LOOKS], part_imag[m % LOOKS]
+    return out_real, out_imag
+
+
+def quadrants(real, imag):
+    return jnp.concatenate(
+        [jnp.concatenate([real, imag], axis=1), jnp.concatenate([imag, -real], axis=1)], axis=0
+    )
+
+
+def block_of(me, r, peers):
+    return (jnp.bitwise_xor(me, r) - me) % peers
+
+
+def product(table, data):
+    return jnp.dot(table, data, preferred_element_type=jnp.float32)
+
+
+def transform(table_ref, tap, real, imag):
+    real_high, real_low = split_pair(real)
+    imag_high, imag_low = split_pair(imag)
+    high, low = quadrants(real_high, imag_high), quadrants(real_low, imag_low)
+    table_high, table_low = table_ref[0, tap], table_ref[1, tap]
+    return product(table_high, high) + product(table_low, high) + product(table_high, low)
+
+
+def tables_kernel(count, *refs):
+    for source, target in zip(refs[:count], refs[count:]):
+        target[...] = source[...]
+
+
+def early_kernel(peers, last, table_ref, *refs):
+    own_refs, sec_refs = refs[:peers], list(refs[peers : 2 * peers - 1])
+    out_ref, real_ref, imag_ref = refs[2 * peers - 1 :]
+    sec_refs.insert(last, None)
+    me = lax.axis_index("line")
+    chunk_lines = own_refs[0].shape[0]
+    inner = peers * chunk_lines // TAPS
+    for r in range(peers):
+        base = pl.multiple_of(block_of(me, r, peers) * chunk_lines, 8)
+        own = own_refs[r][...]
+        mask = low_lanes(own.shape)
+        if r == last:
+            real, imag = jnp.where(mask, own, 0.0), jnp.where(mask, swap_halves(own), 0.0)
+        else:
+            sec = sec_refs[r][...]
+            real, imag = jnp.where(mask, own, swap_halves(sec)), jnp.where(mask, swap_halves(own), sec)
+        real_ref[pl.ds(base, chunk_lines), :] = real
+        imag_ref[pl.ds(base, chunk_lines), :] = imag
+    for l in range(TAPS):
+        span = pl.ds(l, inner, stride=TAPS)
+        out_ref[l] = transform(table_ref, l, real_ref[span, :], imag_ref[span, :])
+
+
+def late_kernel(
+    peers, start_ref, stop_ref, late_ref, back_ref, mid_ref, sec_ref, *refs
+):
+    out_refs = refs[:peers]
+    real_ref, imag_ref, sum_ref = refs[peers:]
     me = lax.axis_index("line")
     date = lax.axis_index("date")
-    chunk_lines = own_refs[0].shape[0]
-    lines_all = peers * chunk_lines
-    for r in range(peers):
-        base = pl.multiple_of(jnp.bitwise_xor(me, r) * chunk_lines, 8)
-        own, sec = own_refs[r][...], sec_refs[r][...]
-        mask = low_lanes(own.shape)
-        real_ref[pl.ds(base, chunk_lines), :] = jnp.where(mask, own, swap_halves(sec))
-        imag_ref[pl.ds(base, chunk_lines), :] = jnp.where(mask, swap_halves(own), sec)
-
-    high_table, low_table = matrix_ref[0], matrix_ref[1]
-
-    def transform(high, low):
-        return (
-            jnp.dot(high_table, high, preferred_element_type=jnp.float32)
-            + jnp.dot(high_table, low, preferred_element_type=jnp.float32)
-            + jnp.dot(low_table, high, preferred_element_type=jnp.float32)
-        )
-
-    for l in range(LOOKS):
-        real_high, real_low = split_pair(real_ref[pl.ds(l, inner, stride=LOOKS), :])
-        imag_high, imag_low = split_pair(imag_ref[pl.ds(l, inner, stride=LOOKS), :])
-        high = jnp.concatenate(
-            [
-                jnp.concatenate([real_high, imag_high], axis=1),
-                jnp.concatenate([imag_high, -real_high], axis=1),
-            ],
-            axis=0,
-        )
-        low = jnp.concatenate(
-            [
-                jnp.concatenate([real_low, imag_low], axis=1),
-                jnp.concatenate([imag_low, -real_low], axis=1),
-            ],
-            axis=0,
-        )
-        mid_ref[l] = transform(high, low)
+    chunk_lines = sec_ref.shape[0]
+    inner = peers * chunk_lines // TAPS
+    few = chunk_lines // TAPS
+    sec = sec_ref[...]
+    mask = low_lanes(sec.shape)
+    real_ref[0:chunk_lines, :] = jnp.where(mask, 0.0, swap_halves(sec))
+    imag_ref[0:chunk_lines, :] = jnp.where(mask, 0.0, sec)
+    for l in range(TAPS):
+        span = pl.ds(l, few, stride=TAPS)
+        real_high, real_low = split_pair(real_ref[span, :])
+        imag_high, imag_low = split_pair(imag_ref[span, :])
+        high, low = quadrants(real_high, imag_high), quadrants(real_low, imag_low)
+        rest = jnp.zeros((late_ref.shape[2] - 6 * few, 2 * LANES), jnp.bfloat16)
+        mid_ref[l] += product(late_ref[l], jnp.concatenate([high, low, high, rest], axis=0))
 
     start, stop = start_ref[date], stop_ref[date]
-    rows = 16
+    width = stop - start
+    rows = 8
 
     def spectral(step, carry):
         row = pl.multiple_of(step * rows, rows)
         span = pl.ds(row, rows)
-        real = [mid_ref[l, span, :LANES] for l in range(LOOKS)]
-        imag = [mid_ref[l, span, LANES:] for l in range(LOOKS)]
-        turn = [(twist_ref[l, 0, span, :], twist_ref[l, 1, span, :]) for l in range(LOOKS - 1)]
-        for l in range(1, LOOKS):
-            c, s = turn[l - 1]
-            real[l], imag[l] = real[l] * c + imag[l] * s, imag[l] * c - real[l] * s
-        real, imag = five_point(real, imag, -1.0)
-        first = lax.broadcasted_iota(jnp.int32, (rows, LANES), 0) + row
-        for m in range(LOOKS):
-            bin_index = first + m * inner
-            keep = (bin_index >= start) & (bin_index < stop)
-            weight = jnp.where(keep, 1.0 / lines_all, 0.0)
-            real[m], imag[m] = real[m] * weight, imag[m] * weight
-        real, imag = five_point(real, imag, 1.0)
-        for l in range(1, LOOKS):
-            c, s = turn[l - 1]
-            real[l], imag[l] = real[l] * c - imag[l] * s, imag[l] * c + real[l] * s
-        span_below = pl.ds(pl.multiple_of(row + inner, rows), rows)
-        for l in range(LOOKS):
-            real_high, real_low = split_pair(real[l])
-            imag_high, imag_low = split_pair(imag[l])
-            high_ref[l, span, :LANES] = real_high
-            high_ref[l, span, LANES:] = imag_high
-            high_ref[l, span_below, :LANES] = -imag_high
-            high_ref[l, span_below, LANES:] = real_high
-            low_ref[l, span, :LANES] = real_low
-            low_ref[l, span, LANES:] = imag_low
-            low_ref[l, span_below, :LANES] = -imag_low
-            low_ref[l, span_below, LANES:] = real_low
+        real = [mid_ref[l, span, :LANES] for l in range(TAPS)]
+        imag = [mid_ref[l, span, LANES:] for l in range(TAPS)]
+        real, imag = ten_point(real, imag, -1.0)
+        first = lax.broadcasted_iota(jnp.int32, (rows, LANES), 0) + (row - start)
+        for m in range(TAPS):
+            offset = first + m * inner
+            keep = (offset >= 0) & (offset < width)
+            real[m], imag[m] = jnp.where(keep, real[m], 0.0), jnp.where(keep, imag[m], 0.0)
+        real, imag = ten_point(real, imag, 1.0)
+        for l in range(TAPS):
+            mid_ref[l, span, :LANES] = real[l]
+            mid_ref[l, span, LANES:] = imag[l]
         return carry
 
     lax.fori_loop(0, inner // rows, spectral, 0)
 
-    total = None
-    for l in range(LOOKS):
-        signal = transform(high_ref[l], low_ref[l])
-        real, imag = signal[:, :LANES], signal[:, LANES:]
-        real_other, imag_other = swap_halves(real), swap_halves(imag)
-        product = jnp.where(
-            low_lanes(real.shape),
-            real * real_other + imag * imag_other,
-            real * imag_other - imag * real_other,
-        )
-        total = product if total is None else total + product
-    sum_ref[...] = total * (1.0 / LOOKS)
-    out_lines = inner // peers
+    lines_all = peers * chunk_lines
+    scale = 1.0 / (lines_all * lines_all * LOOKS)
+    for half in range(2):
+        total = None
+        for l in range(half * LOOKS, (half + 1) * LOOKS):
+            signal = transform(back_ref, l, mid_ref[l, :, :LANES], mid_ref[l, :, LANES:])
+            real, imag = signal[:, :LANES], signal[:, LANES:]
+            real_other, imag_other = swap_halves(real), swap_halves(imag)
+            value = jnp.where(
+                low_lanes(real.shape),
+                real * real_other + imag * imag_other,
+                real * imag_other - imag * real_other,
+            )
+            total = value if total is None else total + value
+        sum_ref[pl.ds(half, inner, stride=2), :] = total * scale
+    out_lines = 2 * inner // peers
     for r in range(peers):
-        base = pl.multiple_of(jnp.bitwise_xor(me, r) * out_lines, 8)
+        base = pl.multiple_of(block_of(me, r, peers) * out_lines, 8)
         out_refs[r][...] = sum_ref[pl.ds(base, out_lines), :]
 
 
@@ -317,8 +359,8 @@
 def packed_step(slc, band_start, band_stop):
     peers = lax.axis_size("line")
     chunk_lines = slc.shape[3]
-    inner = peers * chunk_lines // LOOKS
-    out_lines = inner // peers
+    inner = peers * chunk_lines // TAPS
+    out_lines = 2 * inner // peers
     f32 = jnp.float32
     vmem = pl.BlockSpec(memory_space=pltpu.VMEM)
     smem = pl.BlockSpec(memory_space=pltpu.SMEM)
@@ -341,23 +383,36 @@
 
     own = [values if r == 0 else exchange(values, r) for r, values in enumerate(packed)]
     sec = [forward(values) for values in own]
-    matrix, twist = host_tables(inner)
+    last = peers // 2
+    tables = [jnp.asarray(table) for table in host_tables(inner, chunk_lines, last)]
+    ahead, back, late = pl.pallas_call(
+        functools.partial(tables_kernel, len(tables)),
+        out_shape=[jax.ShapeDtypeStruct(table.shape, table.dtype) for table in tables],
+        in_specs=[vmem] * len(tables),
+        out_specs=[vmem] * len(tables),
+        compiler_params=pltpu.CompilerParams(vmem_limit_bytes=16 * MIB),
+        name="tables",
+    )(*tables)
+    planes = pltpu.VMEM((peers * chunk_lines, LANES), f32)
+    middle = pl.pallas_call(
+        functools.partial(early_kernel, peers, last),
+        out_shape=jax.ShapeDtypeStruct((TAPS, inner, 2 * LANES), f32),
+        in_specs=[vmem] * (2 * peers),
+        out_specs=vmem,
+        scratch_shapes=[planes, planes],
+        compiler_params=pltpu.CompilerParams(vmem_limit_bytes=16 * MIB),
+        name="early",
+    )(ahead, *own, *(values for r, values in enumerate(sec) if r != last))
+    part = pltpu.VMEM((chunk_lines, LANES), f32)
     looked = pl.pallas_call(
-        functools.partial(main_kernel, peers, inner),
+        functools.partial(late_kernel, peers),
         out_shape=[jax.ShapeDtypeStruct((out_lines, LANES), f32)] * peers,
-        in_specs=[smem, smem, vmem, vmem] + [vmem] * (2 * peers),
+        in_specs=[smem, smem] + [vmem] * 4,
         out_specs=[vmem] * peers,
-        scratch_shapes=[
-            pltpu.VMEM((peers * chunk_lines, LANES), f32),
-            pltpu.VMEM((peers * chunk_lines, LANES), f32),
-            pltpu.VMEM((LOOKS, inner, 2 * LANES), f32),
-            pltpu.VMEM((LOOKS, 2 * inner, 2 * LANES), jnp.bfloat16),
-            pltpu.VMEM((LOOKS, 2 * inner, 2 * LANES), jnp.bfloat16),
-            pltpu.VMEM((inner, LANES), f32),
-        ],
-        compiler_params=pltpu.CompilerParams(vmem_limit_bytes=24 * MIB),
-        name="interfere",
-    )(band_start, band_stop, jnp.asarray(matrix), jnp.asarray(twist), *own, *sec)
+        scratch_shapes=[part, part, pltpu.VMEM((2 * inner, LANES), f32)],
+        compiler_params=pltpu.CompilerParams(vmem_limit_bytes=16 * MIB),
+        name="late",
+    )(band_start, band_stop, late, back, middle, sec[last])
     looked = [values if r == 0 else exchange(values, r) for r, values in enumerate(looked)]
     result = pl.pallas_call(
         functools.partial(unpack_kernel, peers),
@@ -374,13 +429,11 @@
     peers = mesh.shape["line"]
     columns = slc.shape[2] // mesh.shape["stack"] // peers
     chunk_lines = slc.shape[3] // peers
-    inner = slc.shape[3] // LOOKS
+    inner = slc.shape[3] // TAPS
     return (
-        peers > 1
-        and peers & (peers - 1) == 0
-        and columns == HALF
-        and chunk_lines % 8 == 0
-        and inner % (8 * peers) == 0
+        columns == HALF
+        and peers == 4
+        and chunk_lines % (16 * TAPS) == 0
         and inner % LANES == 0
         and inner <= 4 * LANES
     )

time: 40 us -> 39.2 us (0.980)
  local copies, waits for them, and re-layouts: 2.32 us -> 4.82 us
  starting transfers between devices: 12.1 us -> 10.6 us
  Pallas kernels: 6.02 us -> 4.86 us
  waiting for transfers between devices: 19.3 us -> 18.5 us
    ppermute x4, waiting for transfers between devices: 2.99 us -> 0.01 us  [shifted(): lax.ppermute(shard, axis, [(i, (i + by) % size) for i in range(size)])]
    unnamed x10 -> x12, local copies, waits for them, and re-layouts: 2.32 us -> 4.82 us
    ppermute x6, waiting for transfers between devices: 16.3 us -> 18.5 us  [exchange(): return lax.ppermute(values, 'line', [(i, i ^ r) for i in range(peers)])]
    ppermute x4, starting transfers between devices: 1.98 us -> 0.45 us  [shifted(): lax.ppermute(shard, axis, [(i, (i + by) % size) for i in range(size)])]
    pallas_call x1 -> x3, Pallas kernels: 5.02 us -> 3.86 us  [the longest x1 2.56 us: packed_step(): pl.pallas_call(functools.partial(late_kernel, peers), out_shape=[jax.Shap...]
  transfers between devices with their start and end apart: 10 -> 10, of which waited for: 6 -> 5; matrix products, arithmetic and copies ran while one was open for 0% -> 0% of each run, Pallas kernels for 0% -> 3%
where the time goes in v1:
time: 39.2 us; the launch traced here: 38.9 us
  waiting for transfers between devices  18.5 us (47%)
  starting transfers between devices  10.6 us (27%)
  Pallas kernels  4.86 us (12%)
  local copies, waits for them, and re-layouts  4.82 us (12%)
    ppermute x6, waiting for transfers between devices, exchange(): return lax.ppermute(values, 'line', [(i, i ^ r) for i in range(peers)])  18.5 us
    ppermute x6, starting transfers between devices, exchange(): return lax.ppermute(values, 'line', [(i, i ^ r) for i in range(peers)])  10.2 us
    unnamed x12, local copies, waits for them, and re-layouts  4.82 us
    pallas_call x1, Pallas kernels, packed_step(): pl.pallas_call(functools.partial(late_kernel, peers), out_shape=[jax.Shap...  2.56 us
    pallas_call x1, Pallas kernels, packed_step(): pl.pallas_call(functools.partial(early_kernel, peers, last), out_shape=ja...  1.09 us
  transfers between devices with their start and end apart: 10, of which 5 were waited for; matrix products, arithmetic and copies ran while one was open for 0% of the time, Pallas kernels for 3%

profile of v1, /device:TPU:0, one launch (start us, length us, event | category | flops | bytes accessed | tf_op | source)
XLA Modules:
  0.0 38.9 jit_solution(16874343848788127075)
XLA Ops:
  0.0 0.0 copy-start.2
  0.0 1.1 %copy-done.2 = f32[1,2,256,320]{2,3,1,0:T(8,128)S(1)} copy-done((f32[1,2,256,320]{2,3,1,0:T(8,128)S(1)}, f32[1,2,256,320]{2,3,1,0:T(8,128)}, u32[]{:S(2)}) %copy-start.2) | copy-done | bytes 655384
  1.1 0.2 pack.1
  1.3 3.1 %collective-permute-start = (f32[320,128]{1,0:T(8,128)S(1)}, f32[320,128]{1,0:T(8,128)S(1)}, u32[]{:S(2)}, u32[]{:S(2)}) collective-permute-start(f32[320,128]{1,0:T(8,128)S(1)} %get-tuple-element.20), channel_id=1, source_target_pairs={{0,1},{1,0},{2,3},{3,2},{4,5},{5,4},{6,7},{7,6},{8,9},{9,8},{10,11... | collective-permute-start | bytes 491528 | tf_op jit(solution)/shard_map/ppermute | solution.py:379
  4.5 2.5 %collective-permute-start.2 = (f32[320,128]{1,0:T(8,128)S(1)}, f32[320,128]{1,0:T(8,128)S(1)}, u32[]{:S(2)}, u32[]{:S(2)}) collective-permute-start(f32[320,128]{1,0:T(8,128)S(1)} %get-tuple-element.22), channel_id=1, source_target_pairs={{0,3},{1,2},{2,1},{3,0},{4,7},{5,6},{6,5},{7,4},{8,11},{9,10},{10,... | collective-permute-start | bytes 491528 | tf_op jit(solution)/shard_map/ppermute | solution.py:379
  6.9 0.1 collective-permute-start.1
  7.0 0.4 collective-permute-start.3
  7.4 1.6 %collective-permute-done.refs_1_ = f32[320,128]{1,0:T(8,128)S(1)} collective-permute-done((f32[320,128]{1,0:T(8,128)S(1)}, f32[320,128]{1,0:T(8,128)S(1)}, u32[]{:S(2)}, u32[]{:S(2)}) %collective-permute-start) | collective-permute-done | bytes 163872 | tf_op jit(solution)/shard_map/ppermute | solution.py:379
  9.0 0.0 collective-permute-start.4
  9.0 6.5 %collective-permute-done.2.refs_3_ = f32[320,128]{1,0:T(8,128)S(1)} collective-permute-done((f32[320,128]{1,0:T(8,128)S(1)}, f32[320,128]{1,0:T(8,128)S(1)}, u32[]{:S(2)}, u32[]{:S(2)}) %collective-permute-start.2) | collective-permute-done | bytes 163872 | tf_op jit(solution)/shard_map/ppermute | solution.py:379
  15.6 0.0 collective-permute-start.5
  15.6 5.9 %collective-permute-done.1.refs_2_ = f32[320,128]{1,0:T(8,128)S(1)} collective-permute-done((f32[320,128]{1,0:T(8,128)S(1)}, f32[320,128]{1,0:T(8,128)S(1)}, u32[]{:S(2)}, u32[]{:S(2)}) %collective-permute-start.1) | collective-permute-done | bytes 163872 | tf_op jit(solution)/shard_map/ppermute | solution.py:379
  21.5 0.1 collective-permute-start.6
  21.6 0.0 copy-start
  21.6 1.3 %copy-done = bf16[2,10,128,256]{3,2,1,0:T(8,128)(2,1)S(1)} copy-done((bf16[2,10,128,256]{3,2,1,0:T(8,128)(2,1)S(1)}, bf16[2,10,128,256]{3,2,1,0:T(8,128)(2,1)}, u32[]{:S(2)}) %copy-start) | copy-done | bytes 1310744
  22.9 0.0 copy-start.1
  22.9 1.3 %copy-done.1 = bf16[2,10,128,256]{3,2,1,0:T(8,128)(2,1)S(1)} copy-done((bf16[2,10,128,256]{3,2,1,0:T(8,128)(2,1)S(1)}, bf16[2,10,128,256]{3,2,1,0:T(8,128)(2,1)}, u32[]{:S(2)}) %copy-start.1) | copy-done | bytes 1310744
  24.2 0.0 copy-start.3
  24.2 1.1 %copy-done.3 = bf16[10,128,256]{2,1,0:T(8,128)(2,1)S(1)} copy-done((bf16[10,128,256]{2,1,0:T(8,128)(2,1)S(1)}, bf16[10,128,256]{2,1,0:T(8,128)(2,1)}, u32[]{:S(2)}) %copy-start.3) | copy-done | bytes 655384
  25.3 0.2 tables.1
  25.5 0.0 collective-permute-done.3.refs_4_
  25.5 0.0 collective-permute-done.4.refs_5_
  25.5 0.0 collective-permute-done.5.refs_6_
  25.5 0.0 copy-start.4
  25.5 0.0 copy-start.5
  25.6 1.1 %early.1.mid_ref = f32[10,128,256]{2,1,0:T(8,128)S(1)} custom-call(bf16[2,10,128,256]{3,2,1,0:T(8,128)(2,1)S(1)} %get-tuple-element.18.table_ref, f32[320,128]{1,0:T(8,128)S(1)} %get-tuple-element.19.refs_0_, f32[320,128]{1,0:T(8,128)S(1)} %collective-permute-done.refs_1_, f32[320,128]{1,0:T(8,128)S(1)} %collective-permute-done.1.refs_2_, ...), custom_call_target="tpu_custom_call" | custom-call | tf_op jit(solution)/shard_map/early/pallas_call | solution.py:397
  26.6 0.0 collective-permute-done.6.sec_ref
  26.7 0.0 copy-done.4
  26.7 0.0 copy-done.5
  26.7 2.6 %late.1 = (f32[64,128]{1,0:T(8,128)S(1)}, f32[64,128]{1,0:T(8,128)S(1)}, f32[64,128]{1,0:T(8,128)S(1)}, f32[64,128]{1,0:T(8,128)S(1)}) custom-call(s32[4]{0:T(128)S(1)} %copy-done.4, s32[4]{0:T(128)S(1)} %copy-done.5, bf16[10,128,256]{2,1,0:T(8,128)(2,1)S(1)} %get-tuple-element.16.late_ref, bf16[2,10,128,256]{3,2,1,0:T(8,128)(2,1)S(1)} %get-tuple-element.17.back_ref, ...), custom_call_target="tpu_custom_call" | custom-call | tf_op jit(solution)/shard_map/late/pallas_call | solution.py:407
  29.2 0.1 collective-permute-start.7
  29.3 3.1 %collective-permute-start.8 = (f32[64,128]{1,0:T(8,128)S(1)}, f32[64,128]{1,0:T(8,128)S(1)}, u32[]{:S(2)}, u32[]{:S(2)}) collective-permute-start(f32[64,128]{1,0:T(8,128)S(1)} %get-tuple-element.25), channel_id=1, source_target_pairs={{0,2},{1,3},{2,0},{3,1},{4,6},{5,7},{6,4},{7,5},{8,10},{9,11},{10,... | collective-permute-start | bytes 98312 | tf_op jit(solution)/shard_map/ppermute | solution.py:379
  32.4 1.3 %collective-permute-start.9 = (f32[64,128]{1,0:T(8,128)S(1)}, f32[64,128]{1,0:T(8,128)S(1)}, u32[]{:S(2)}, u32[]{:S(2)}) collective-permute-start(f32[64,128]{1,0:T(8,128)S(1)} %get-tuple-element.26), channel_id=1, source_target_pairs={{0,3},{1,2},{2,1},{3,0},{4,7},{5,6},{6,5},{7,4},{8,11},{9,10},{10,... | collective-permute-start | bytes 98312 | tf_op jit(solution)/shard_map/ppermute | solution.py:379
  33.7 0.0 collective-permute-done.7.refs_1_
  33.7 0.6 %collective-permute-done.8.refs_2_ = f32[64,128]{1,0:T(8,128)S(1)} collective-permute-done((f32[64,128]{1,0:T(8,128)S(1)}, f32[64,128]{1,0:T(8,128)S(1)}, u32[]{:S(2)}, u32[]{:S(2)}) %collective-permute-start.8) | collective-permute-done | bytes 32800 | tf_op jit(solution)/shard_map/ppermute | solution.py:379
  34.3 3.8 %collective-permute-done.9.refs_3_ = f32[64,128]{1,0:T(8,128)S(1)} collective-permute-done((f32[64,128]{1,0:T(8,128)S(1)}, f32[64,128]{1,0:T(8,128)S(1)}, u32[]{:S(2)}, u32[]{:S(2)}) %collective-permute-start.9) | collective-permute-done | bytes 32800 | tf_op jit(solution)/shard_map/ppermute | solution.py:379
  38.2 0.8 %unpack.1 = f32[2,64,256]{2,1,0:T(8,128)} custom-call(f32[64,128]{1,0:T(8,128)S(1)} %get-tuple-element.23.refs_0_, f32[64,128]{1,0:T(8,128)S(1)} %collective-permute-done.7.refs_1_, f32[64,128]{1,0:T(8,128)S(1)} %collective-permute-done.8.refs_2_, f32[64,128]{1,0:T(8,128)S(1)} %collective-permute-done.9.refs_3_), custom_call_target="tpu_custom_call" | custom-call | tf_op jit(solution)/shard_map/unpack/pallas_call | solution.py:417
Async XLA Ops:
  0.0 1.1 %copy-start.2 = (f32[1,2,256,320]{2,3,1,0:T(8,128)S(1)}, f32[1,2,256,320]{2,3,1,0:T(8,128)}, u32[]{:S(2)}) copy-start(f32[1,2,256,320]{2,3,1,0:T(8,128)} %param.6) | copy-start | bytes 1966084
  1.3 7.7 %collective-permute-start = (f32[320,128]{1,0:T(8,128)S(1)}, f32[320,128]{1,0:T(8,128)S(1)}, u32[]{:S(2)}, u32[]{:S(2)}) collective-permute-start(f32[320,128]{1,0:T(8,128)S(1)} %get-tuple-element.20), channel_id=1, source_target_pairs={{0,1},{1,0},{2,3},{3,2},{4,5},{5,4},{6,7},{7,6},{8,9},{9,8},{10,11... | collective-permute-start | bytes 491528 | tf_op jit(solution)/shard_map/ppermute | solution.py:379
  4.5 11.1 %collective-permute-start.2 = (f32[320,128]{1,0:T(8,128)S(1)}, f32[320,128]{1,0:T(8,128)S(1)}, u32[]{:S(2)}, u32[]{:S(2)}) collective-permute-start(f32[320,128]{1,0:T(8,128)S(1)} %get-tuple-element.22), channel_id=1, source_target_pairs={{0,3},{1,2},{2,1},{3,0},{4,7},{5,6},{6,5},{7,4},{8,11},{9,10},{10,... | collective-permute-start | bytes 491528 | tf_op jit(solution)/shard_map/ppermute | solution.py:379
  6.9 14.6 %collective-permute-start.1 = (f32[320,128]{1,0:T(8,128)S(1)}, f32[320,128]{1,0:T(8,128)S(1)}, u32[]{:S(2)}, u32[]{:S(2)}) collective-permute-start(f32[320,128]{1,0:T(8,128)S(1)} %get-tuple-element.21), channel_id=1, source_target_pairs={{0,2},{1,3},{2,0},{3,1},{4,6},{5,7},{6,4},{7,5},{8,10},{9,11},{10,... | collective-permute-start | bytes 491528 | tf_op jit(solution)/shard_map/ppermute | solution.py:379
  7.0 18.5 %collective-permute-start.3 = (f32[320,128]{1,0:T(8,128)S(1)}, f32[320,128]{1,0:T(8,128)S(1)}, u32[]{:S(2)}, u32[]{:S(2)}) collective-permute-start(f32[320,128]{1,0:T(8,128)S(1)} %get-tuple-element.19.refs_0_), channel_id=1, source_target_pairs={{0,12},{4,0},{8,4},{12,8},{1,13},{5,1},{9,5},{13,9},{2,14},{6,2},{... | collective-permute-start | bytes 491528 | tf_op jit(solution)/shard_map/ppermute | solution.py:25
  9.0 16.5 %collective-permute-start.4 = (f32[320,128]{1,0:T(8,128)S(1)}, f32[320,128]{1,0:T(8,128)S(1)}, u32[]{:S(2)}, u32[]{:S(2)}) collective-permute-start(f32[320,128]{1,0:T(8,128)S(1)} %collective-permute-done.refs_1_), channel_id=1, source_target_pairs={{0,12},{4,0},{8,4},{12,8},{1,13},{5,1},{9,5},{13,9},{2,14},{6,2},{... | collective-permute-start | bytes 491528 | tf_op jit(solution)/shard_map/ppermute | solution.py:25
  15.6 9.9 %collective-permute-start.5 = (f32[320,128]{1,0:T(8,128)S(1)}, f32[320,128]{1,0:T(8,128)S(1)}, u32[]{:S(2)}, u32[]{:S(2)}) collective-permute-start(f32[320,128]{1,0:T(8,128)S(1)} %collective-permute-done.2.refs_3_), channel_id=1, source_target_pairs={{0,12},{4,0},{8,4},{12,8},{1,13},{5,1},{9,5},{13,9},{2,14},{6,2},{... | collective-permute-start | bytes 491528 | tf_op jit(solution)/shard_map/ppermute | solution.py:25
  21.5 5.2 %collective-permute-start.6 = (f32[320,128]{1,0:T(8,128)S(1)}, f32[320,128]{1,0:T(8,128)S(1)}, u32[]{:S(2)}, u32[]{:S(2)}) collective-permute-start(f32[320,128]{1,0:T(8,128)S(1)} %collective-permute-done.1.refs_2_), channel_id=1, source_target_pairs={{0,12},{4,0},{8,4},{12,8},{1,13},{5,1},{9,5},{13,9},{2,14},{6,2},{... | collective-permute-start | bytes 491528 | tf_op jit(solution)/shard_map/ppermute | solution.py:25
  21.6 1.3 %copy-start = (bf16[2,10,128,256]{3,2,1,0:T(8,128)(2,1)S(1)}, bf16[2,10,128,256]{3,2,1,0:T(8,128)(2,1)}, u32[]{:S(2)}) copy-start(bf16[2,10,128,256]{3,2,1,0:T(8,128)(2,1)} %constant.6.clone.refs_0_) | copy-start | bytes 3932164
  22.9 1.3 %copy-start.1 = (bf16[2,10,128,256]{3,2,1,0:T(8,128)(2,1)S(1)}, bf16[2,10,128,256]{3,2,1,0:T(8,128)(2,1)}, u32[]{:S(2)}) copy-start(bf16[2,10,128,256]{3,2,1,0:T(8,128)(2,1)} %constant.7.clone.refs_1_) | copy-start | bytes 3932164
  24.2 1.1 %copy-start.3 = (bf16[10,128,256]{2,1,0:T(8,128)(2,1)S(1)}, bf16[10,128,256]{2,1,0:T(8,128)(2,1)}, u32[]{:S(2)}) copy-start(bf16[10,128,256]{2,1,0:T(8,128)(2,1)} %constant.8.clone.refs_2_) | copy-start | bytes 1966084
  25.5 1.1 %copy-start.4 = (s32[4]{0:T(128)S(1)}, s32[4]{0:T(128)}, u32[]{:S(2)}) copy-start(s32[4]{0:T(128)} %start_ref.1) | copy-start | bytes 52
  25.5 1.1 %copy-start.5 = (s32[4]{0:T(128)S(1)}, s32[4]{0:T(128)}, u32[]{:S(2)}) copy-start(s32[4]{0:T(128)} %stop_ref.1) | copy-start | bytes 52
  29.2 4.5 %collective-permute-start.7 = (f32[64,128]{1,0:T(8,128)S(1)}, f32[64,128]{1,0:T(8,128)S(1)}, u32[]{:S(2)}, u32[]{:S(2)}) collective-permute-start(f32[64,128]{1,0:T(8,128)S(1)} %get-tuple-element.24), channel_id=1, source_target_pairs={{0,1},{1,0},{2,3},{3,2},{4,5},{5,4},{6,7},{7,6},{8,9},{9,8},{10,11... | collective-permute-start | bytes 98312 | tf_op jit(solution)/shard_map/ppermute | solution.py:379
  29.3 5.0 %collective-permute-start.8 = (f32[64,128]{1,0:T(8,128)S(1)}, f32[64,128]{1,0:T(8,128)S(1)}, u32[]{:S(2)}, u32[]{:S(2)}) collective-permute-start(f32[64,128]{1,0:T(8,128)S(1)} %get-tuple-element.25), channel_id=1, source_target_pairs={{0,2},{1,3},{2,0},{3,1},{4,6},{5,7},{6,4},{7,5},{8,10},{9,11},{10,... | collective-permute-start | bytes 98312 | tf_op jit(solution)/shard_map/ppermute | solution.py:379
  32.4 5.7 %collective-permute-start.9 = (f32[64,128]{1,0:T(8,128)S(1)}, f32[64,128]{1,0:T(8,128)S(1)}, u32[]{:S(2)}, u32[]{:S(2)}) collective-permute-start(f32[64,128]{1,0:T(8,128)S(1)} %get-tuple-element.26), channel_id=1, source_target_pairs={{0,3},{1,2},{2,1},{3,0},{4,7},{5,6},{6,5},{7,4},{8,11},{9,10},{10,... | collective-permute-start | bytes 98312 | tf_op jit(solution)/shard_map/ppermute | solution.py:379
